TPU v7x, 32 devices: a whole 2x2x4 slice. The times are simulated.
32 devices in a mesh: dp: 2 (over y), seq: 16 (over z, x, core).
Axes of the slice: x: 2, y: 2, z: 4, core: 2. Of those that a mesh axis runs over, the one named last changes fastest.
Arguments:
- tokens: bfloat16 [2, 8192, 1024], P('dp', 'seq'), may hold values from -18 to 18
- lengths: int32 [2, 64], P('dp'), may hold values from 1 to 128
- w_query: bfloat16 [1024, 512], replicated, may hold values from -0.1875 to 0.1875
- w_key: bfloat16 [1024, 512], replicated, may hold values from -0.1875 to 0.1875
- w_value: bfloat16 [1024, 512], replicated, may hold values from -0.1875 to 0.1875
- w_out: bfloat16 [512, 1024], replicated, may hold values from -2 to 2
- cotangent: bfloat16 [2, 8192, 1024], P('dp', 'seq'), may hold values from -6 to 6
Outputs:
- mixed: bfloat16 [2, 8192, 1024], P('dp', 'seq')
- grad_tokens: bfloat16 [2, 8192, 1024], P('dp', 'seq')
- grad_query: float32 [1024, 512], replicated
- grad_key: float32 [1024, 512], replicated
- grad_value: float32 [1024, 512], replicated
- grad_output: float32 [512, 1024], replicated
All inputs are finite; a program needn't handle non-finite values.
Results may differ from a plain program's by a relative error of at most 0.014.
The roundings to bfloat16 on the way count: a program that leaves them out, or rounds other values in their place, can miss the bound.
Values may be sent and summed in bfloat16 or wider, within the bound.
No kernel may reach another device: no remote copies, remote signals or barrier semaphores. Data moves between devices by JAX's collectives and lax.ppermute only.
A program may use at most 192 MiB of HBM per device.

v0:
```python
import math
import jax
import jax.numpy as jnp
from jax import lax
from jax.sharding import PartitionSpec as P

HEADS = 4
TILE = 128
bar_offsets = (0, 1, 2, 4, 8, 12, 16, 24, 32)
group_bars = 4
far_score = -1e30


def shifted(block, axis, distance):
    devices = range(lax.axis_size(axis))
    route = [(i - distance, i) for i in devices if i - distance in devices]
    return lax.ppermute(block, axis, route)


def product(form, left, right):
    return jnp.einsum(form, left, right, preferred_element_type=jnp.float32)


def summarize(bar_rows, length):
    slot_ids = jnp.arange(bar_rows.shape[1], dtype=jnp.int32)
    live_slots = slot_ids[None, :] < length[:, None]
    running = jnp.sum(jnp.where(live_slots[:, :, None], bar_rows.astype(jnp.float32), 0.0), axis=1)
    return (running / length[:, None].astype(jnp.float32)).astype(jnp.bfloat16)


def bar_block(
    queries,
    ext_key,
    ext_value,
    ext_length,
    base_bar,
    bar_ids,
    query_length,
    summary_key,
    summary_value,
    grad_context,
):
    group_count, tile_len, head_count, head_dim = queries.shape
    sources = len(bar_offsets)
    key_parts = []
    value_parts = []
    length_parts = []
    for offset in bar_offsets:
        first_bar = base_bar - offset
        key_parts.append(lax.dynamic_slice_in_dim(ext_key, first_bar, group_count, 0))
        value_parts.append(lax.dynamic_slice_in_dim(ext_value, first_bar, group_count, 0))
        length_parts.append(lax.dynamic_slice_in_dim(ext_length, first_bar, group_count, 0))
    fine_key = jnp.stack(key_parts, 1).reshape(
        group_count, sources * tile_len, head_count, head_dim
    )
    fine_value = jnp.stack(value_parts, 1).reshape(
        group_count, sources * tile_len, head_count, head_dim
    )
    fine_length = jnp.stack(length_parts, 1)
    slot_ids = jnp.arange(tile_len, dtype=jnp.int32)
    key_live = slot_ids[None, None, :] < fine_length[:, :, None]
    causal = slot_ids[None, :] <= slot_ids[:, None]
    other_bar = jnp.arange(sources, dtype=jnp.int32) != 0
    fine_live = key_live[:, None, :, :] & (
        causal[None, :, None, :] | other_bar[None, None, :, None]
    )
    fine_live = fine_live.reshape(group_count, 1, tile_len, sources * tile_len)
    distance = bar_ids[:, None] - jnp.arange(summary_key.shape[0], dtype=jnp.int32)[None, :]
    coarse_live = distance >= 1
    for offset in bar_offsets[1:]:
        coarse_live = coarse_live & (distance != offset)
    coarse_live = coarse_live[:, None, None, :]
    score_scale = 1.0 / math.sqrt(head_dim)
    fine_score = product("gqhe,gkhe->ghqk", queries, fine_key) * score_scale
    coarse_score = product("gqhe,nhe->ghqn", queries, summary_key) * score_scale
    fine_score = jnp.where(fine_live, fine_score, far_score)
    coarse_score = jnp.where(coarse_live, coarse_score, far_score)
    top_score = jnp.maximum(jnp.max(fine_score, axis=-1), jnp.max(coarse_score, axis=-1))[..., None]
    fine_exp = jnp.where(fine_live, jnp.exp(fine_score - top_score), 0.0)
    coarse_exp = jnp.where(coarse_live, jnp.exp(coarse_score - top_score), 0.0)
    denominator = (jnp.sum(fine_exp, axis=-1) + jnp.sum(coarse_exp, axis=-1))[..., None]
    fine_prob = fine_exp / denominator
    coarse_prob = coarse_exp / denominator
    fine_round = fine_prob.astype(jnp.bfloat16)
    coarse_round = coarse_prob.astype(jnp.bfloat16)
    attended_context = product("ghqk,gkhe->gqhe", fine_round, fine_value) + product(
        "ghqn,nhe->gqhe", coarse_round, summary_value
    )
    query_live = slot_ids[None, :] < query_length[:, None]
    attended_context = jnp.where(query_live[:, :, None, None], attended_context, 0.0)
    fine_dp = product("gqhe,gkhe->ghqk", grad_context, fine_value)
    coarse_dp = product("gqhe,nhe->ghqn", grad_context, summary_value)
    delta = (jnp.sum(fine_prob * fine_dp, axis=-1) + jnp.sum(coarse_prob * coarse_dp, axis=-1))[
        ..., None
    ]
    fine_ds = (fine_prob * (fine_dp - delta) * score_scale).astype(jnp.bfloat16)
    coarse_ds = (coarse_prob * (coarse_dp - delta) * score_scale).astype(jnp.bfloat16)
    query_gradient_rows = product("ghqk,gkhe->gqhe", fine_ds, fine_key) + product(
        "ghqn,nhe->gqhe", coarse_ds, summary_key
    )
    fine_gk = product("ghqk,gqhe->gkhe", fine_ds, queries).reshape(
        group_count, sources, tile_len, head_count, head_dim
    )
    fine_gv = product("ghqk,gqhe->gkhe", fine_round, grad_context).reshape(
        group_count, sources, tile_len, head_count, head_dim
    )
    coarse_key_gradient = product("ghqn,gqhe->nhe", coarse_ds, queries)
    coarse_value_gradient = product("ghqn,gqhe->nhe", coarse_round, grad_context)
    return (
        attended_context,
        query_gradient_rows,
        fine_gk,
        fine_gv,
        coarse_key_gradient,
        coarse_value_gradient,
    )


def spread(running, grads, base_bar):
    group_count = grads.shape[0]
    for position, offset in enumerate(bar_offsets):
        first_bar = base_bar - offset
        current = lax.dynamic_slice_in_dim(running, first_bar, group_count, 0)
        running = lax.dynamic_update_slice_in_dim(
            running, current + grads[:, position], first_bar, 0
        )
    return running


def local(tokens, lengths, w_query, w_key, w_value, w_out, cotangent):
    inputs = tokens[0]
    grad_out = cotangent[0]
    token_count = inputs.shape[0]
    inner_width = w_query.shape[1]
    head_dim = inner_width // HEADS
    bar_count = token_count // TILE
    reach_dev = max(bar_offsets[-1] // bar_count, 1)
    queries = jnp.dot(inputs, w_query, preferred_element_type=jnp.float32).astype(jnp.bfloat16)
    keys_own = jnp.dot(inputs, w_key, preferred_element_type=jnp.float32).astype(jnp.bfloat16)
    values_own = jnp.dot(inputs, w_value, preferred_element_type=jnp.float32).astype(jnp.bfloat16)
    all_length = lengths[0]
    first_own = lax.axis_index("seq") * bar_count
    local_length = lax.dynamic_slice_in_dim(all_length, first_own, bar_count, 0)
    slot_ids = jnp.arange(TILE, dtype=jnp.int32)
    live_slots = slot_ids[None, :] < local_length[:, None]
    token_live = live_slots.reshape(-1)
    own_summary = (
        summarize(keys_own.reshape(bar_count, TILE, inner_width), local_length),
        summarize(values_own.reshape(bar_count, TILE, inner_width), local_length),
    )
    summary_key, summary_value = (
        lax.all_gather(own_summary[0], "seq", axis=0, tiled=True),
        lax.all_gather(own_summary[1], "seq", axis=0, tiled=True),
    )
    summary_key = summary_key.reshape(-1, HEADS, head_dim)
    summary_value = summary_value.reshape(-1, HEADS, head_dim)
    grad_context = jnp.dot(grad_out, w_out.T, preferred_element_type=jnp.float32)
    grad_context = jnp.where(token_live[:, None], grad_context, 0.0).astype(jnp.bfloat16)
    key_stack = keys_own[None]
    value_stack = values_own[None]
    for level_bit in range(reach_dev.bit_length() - 1):
        arrived = shifted((key_stack, value_stack), "seq", 1 << level_bit)
        key_stack = jnp.concatenate([key_stack, arrived[0]], 0)
        value_stack = jnp.concatenate([value_stack, arrived[1]], 0)
    arrived = shifted((key_stack[:1], value_stack[:1]), "seq", reach_dev)
    key_stack = jnp.concatenate([key_stack, arrived[0]], 0)
    value_stack = jnp.concatenate([value_stack, arrived[1]], 0)
    ext_bars = (reach_dev + 1) * bar_count
    ext_key = key_stack[::-1].reshape(ext_bars, TILE, HEADS, head_dim)
    ext_value = value_stack[::-1].reshape(ext_bars, TILE, HEADS, head_dim)
    padded_length = jnp.concatenate([jnp.zeros((reach_dev * bar_count,), jnp.int32), all_length], 0)
    ext_length = lax.dynamic_slice_in_dim(padded_length, first_own, ext_bars, 0)
    query_bars = queries.reshape(bar_count, TILE, HEADS, head_dim)
    grad_bars = grad_context.reshape(bar_count, TILE, HEADS, head_dim)

    def step(carried_state, block_index):
        accumulated_key, accumulated_value, accumulated_summary_key, accumulated_summary_value = (
            carried_state
        )
        begin_bar = block_index * group_bars
        base_bar = reach_dev * bar_count + begin_bar
        bar_ids = first_own + begin_bar + jnp.arange(group_bars, dtype=jnp.int32)
        result = bar_block(
            query_bars,
            ext_key,
            ext_value,
            ext_length,
            base_bar,
            bar_ids,
            local_length,
            summary_key,
            summary_value,
            grad_bars,
        )
        (
            attended_context,
            query_gradient_rows,
            fine_gk,
            fine_gv,
            coarse_key_gradient,
            coarse_value_gradient,
        ) = result
        accumulated_key = spread(accumulated_key, fine_gk, base_bar)
        accumulated_value = spread(accumulated_value, fine_gv, base_bar)
        return (
            (
                accumulated_key,
                accumulated_value,
                accumulated_summary_key + coarse_key_gradient,
                accumulated_summary_value + coarse_value_gradient,
            ),
            (attended_context.astype(jnp.bfloat16), query_gradient_rows.astype(jnp.bfloat16)),
        )

    ext_zero = jnp.zeros((ext_bars, TILE, HEADS, head_dim), jnp.float32)
    sum_zero = jnp.zeros(summary_key.shape, jnp.float32)
    carried_state, stacked = lax.scan(
        step,
        (ext_zero, ext_zero, sum_zero, sum_zero),
        jnp.arange(bar_count // group_bars, dtype=jnp.int32),
    )
    accumulated_key, accumulated_value, accumulated_summary_key, accumulated_summary_value = (
        carried_state
    )
    attended_context = stacked[0].reshape(token_count, inner_width)
    query_gradient_rows = stacked[1].reshape(token_count, inner_width)
    grad_key_stack = accumulated_key.reshape(reach_dev + 1, token_count, inner_width)[::-1]
    grad_value_stack = accumulated_value.reshape(reach_dev + 1, token_count, inner_width)[::-1]
    returned = (
        shifted(grad_key_stack[reach_dev:].astype(jnp.bfloat16), "seq", -reach_dev).astype(
            jnp.float32
        ),
        shifted(grad_value_stack[reach_dev:].astype(jnp.bfloat16), "seq", -reach_dev).astype(
            jnp.float32
        ),
    )
    grad_key_stack = grad_key_stack.at[0:1].add(returned[0])
    grad_value_stack = grad_value_stack.at[0:1].add(returned[1])
    for level_bit in reversed(range(reach_dev.bit_length() - 1)):
        half_span = 1 << level_bit
        returned = (
            shifted(
                grad_key_stack[half_span : 2 * half_span].astype(jnp.bfloat16), "seq", -half_span
            ).astype(jnp.float32),
            shifted(
                grad_value_stack[half_span : 2 * half_span].astype(jnp.bfloat16), "seq", -half_span
            ).astype(jnp.float32),
        )
        grad_key_stack = grad_key_stack.at[:half_span].add(returned[0])
        grad_value_stack = grad_value_stack.at[:half_span].add(returned[1])
    own_key = grad_key_stack[0]
    own_value = grad_value_stack[0]
    summary_back = (
        lax.psum_scatter(
            accumulated_summary_key.astype(jnp.bfloat16), "seq", scatter_dimension=0, tiled=True
        ).astype(jnp.float32),
        lax.psum_scatter(
            accumulated_summary_value.astype(jnp.bfloat16), "seq", scatter_dimension=0, tiled=True
        ).astype(jnp.float32),
    )
    inverse_denominator = 1.0 / local_length.astype(jnp.float32)
    shared_key_rows = summary_back[0].reshape(bar_count, inner_width) * inverse_denominator[:, None]
    share_value = summary_back[1].reshape(bar_count, inner_width) * inverse_denominator[:, None]
    own_key = own_key.reshape(bar_count, TILE, inner_width) + jnp.where(
        live_slots[:, :, None], shared_key_rows[:, None, :], 0.0
    )
    own_value = own_value.reshape(bar_count, TILE, inner_width) + jnp.where(
        live_slots[:, :, None], share_value[:, None, :], 0.0
    )
    grad_keys = own_key.reshape(token_count, inner_width).astype(jnp.bfloat16)
    grad_values = own_value.reshape(token_count, inner_width).astype(jnp.bfloat16)
    mixed = jnp.dot(attended_context, w_out, preferred_element_type=jnp.float32).astype(
        jnp.bfloat16
    )
    grad_in = (
        product("te,de->td", query_gradient_rows, w_query)
        + product("te,de->td", grad_keys, w_key)
        + product("te,de->td", grad_values, w_value)
    )
    weight_terms = (
        product("td,te->de", inputs, query_gradient_rows),
        product("td,te->de", inputs, grad_keys),
        product("td,te->de", inputs, grad_values),
        product("te,td->ed", attended_context, grad_out),
    )
    summed = lax.psum(
        (weight_terms[0], weight_terms[1], weight_terms[2], weight_terms[3]), ("dp", "seq")
    )
    return (
        mixed[None],
        grad_in.astype(jnp.bfloat16)[None],
        summed[0],
        summed[1],
        summed[2],
        summed[3],
    )


def solution(mesh):
    placed = (P("dp", "seq", None), P("dp", None), P(), P(), P(), P(), P("dp", "seq", None))
    return jax.shard_map(
        local,
        mesh=mesh,
        in_specs=placed,
        out_specs=(P("dp", "seq", None), P("dp", "seq", None), P(), P(), P(), P()),
        check_vma=False,
    )
```

profile of v0, /device:TPU:0, one launch (start us, length us, event | category | flops | bytes accessed | tf_op | source)
XLA Modules:
  0.0 892.1 jit_solution(2226027036387687723)
XLA Ops:
  11.3 6.8 collective-permute-start.7
  36.9 22.4 %all-gather = bf16[16,4,512]{2,1,0:T(4,128)(2,1)S(1)} all-gather(bf16[1,4,512]{2,1,0:T(4,128)(2,1)S(1)} %get-tuple-element.209), channel_id=1, replica_groups=mesh['dp'=2,'seq'=16] {'seq'}, dimensions={0}, use_global_device_ids=true | all-gather | bytes 69632 | tf_op jit(solution)/shard_map/all_gather | solution.py:152
  71.9 26.4 %collective-permute-start.1 = (bf16[2,512,512]{2,1,0:T(8,128)(2,1)}, bf16[2,512,512]{2,1,0:T(8,128)(2,1)}, u32[]{:S(2)}, u32[]{:S(2)}) collective-permute-start(bf16[2,512,512]{2,1,0:T(8,128)(2,1)} %pad_maximum_fusion.2), channel_id=1, source_target_pairs={{0,2},{1,3},{2,4},{3,5},{4,6},{5,7},{6,8},{7,9},{8,10},{9,11},{10,... | collective-permute-start | bytes 3145736 | tf_op jit(solution)/shard_map/ppermute | solution.py:17
  100.8 20.4 %collective-permute-start.6 = (bf16[4,512,512]{2,1,0:T(8,128)(2,1)}, bf16[4,512,512]{2,1,0:T(8,128)(2,1)}, u32[]{:S(2)}, u32[]{:S(2)}) collective-permute-start(bf16[4,512,512]{2,1,0:T(8,128)(2,1)} %pad_maximum_fusion.1), channel_id=1, source_target_pairs={{0,4},{1,5},{2,6},{3,7},{4,8},{5,9},{6,10},{7,11},{8,12},{9,13},{1... | collective-permute-start | bytes 6291464 | tf_op jit(solution)/shard_map/ppermute | solution.py:17
  128.3 63.2 %all-gather.1 = bf16[16,4,512]{2,1,0:T(4,128)(2,1)S(1)} all-gather(bf16[1,4,512]{2,1,0:T(4,128)(2,1)S(1)} %get-tuple-element.208), channel_id=1, replica_groups=mesh['dp'=2,'seq'=16] {'seq'}, dimensions={0}, use_global_device_ids=true | all-gather | bytes 69632 | tf_op jit(solution)/shard_map/all_gather | solution.py:153
  234.9 8.2 reshape.634
  275.9 7.7 reshape.631
  297.3 6.0 convolution_bitcast_fusion
  307.0 6.5 multiply_reduce_fusion
  313.6 9.6 %copy.235 = f32[4,1152,4,128]{3,1,2,0:T(8,128)} copy(f32[4,1152,4,128]{1,3,2,0:T(8,128)} %convolution_bitcast_fusion) | data formatting | bytes 18874368 | tf_op jit(solution)/shard_map/while/body/eval_jaxpr/ghqk,gqhe->gkhe/transpose | solution.py:21
  326.8 8.2 multiply_convert_fusion
  342.2 9.6 %copy.221 = f32[4,1152,4,128]{3,1,2,0:T(8,128)} copy(f32[4,1152,4,128]{1,3,2,0:T(8,128)} %convolution_bitcast_fusion.1) | data formatting | bytes 18874368 | tf_op jit(solution)/shard_map/while/body/eval_jaxpr/ghqk,gqhe->gkhe/transpose | solution.py:21
  397.3 15.6 %copy.230 = f32[36,128,4,128]{3,2,1,0:T(4,128)} copy(f32[36,128,4,128]{3,1,2,0:T(8,128)} %constant_dynamic-update-slice_fusion.18) | data formatting | bytes 18874368 | tf_op jit(solution)/shard_map/while/body/eval_jaxpr/dynamic_update_slice | solution.py:124
  415.3 16.0 %copy.244 = f32[36,128,4,128]{3,2,1,0:T(4,128)} copy(f32[36,128,4,128]{3,1,2,0:T(8,128)} %constant_dynamic-update-slice_fusion.17) | data formatting | bytes 18874368 | tf_op jit(solution)/shard_map/while/body/eval_jaxpr/dynamic_update_slice | solution.py:124
  431.3 12.3 %reshape.642 = f32[9,512,512]{2,1,0:T(8,128)} reshape(f32[36,128,4,128]{3,2,1,0:T(4,128)} %copy.230) | data formatting | bytes 18874368 | tf_op jit(solution)/shard_map/reshape | solution.py:227
  443.6 8.4 rev.14
  457.5 12.3 %reshape.647 = f32[9,512,512]{2,1,0:T(8,128)} reshape(f32[36,128,4,128]{3,2,1,0:T(4,128)} %copy.244) | data formatting | bytes 18874368 | tf_op jit(solution)/shard_map/reshape | solution.py:228
  469.7 8.4 rev.15
  495.5 7.2 fusion.11
  510.6 27.8 %collective-permute-done.9 = bf16[4,512,512]{2,1,0:T(8,128)(2,1)} collective-permute-done((bf16[4,512,512]{2,1,0:T(8,128)(2,1)}, bf16[4,512,512]{2,1,0:T(8,128)(2,1)}, u32[]{:S(2)}, u32[]{:S(2)}) %collective-permute-start.9) | collective-permute-done | bytes 2097184 | tf_op jit(solution)/shard_map/ppermute | solution.py:17
  544.9 38.5 %collective-permute-done.13 = bf16[4,512,512]{2,1,0:T(8,128)(2,1)} collective-permute-done((bf16[4,512,512]{2,1,0:T(8,128)(2,1)}, bf16[4,512,512]{2,1,0:T(8,128)(2,1)}, u32[]{:S(2)}, u32[]{:S(2)}) %collective-permute-start.13) | collective-permute-done | bytes 2097184 | tf_op jit(solution)/shard_map/ppermute | solution.py:17
  599.4 16.8 %collective-permute-done.14 = bf16[2,512,512]{2,1,0:T(8,128)(2,1)} collective-permute-done((bf16[2,512,512]{2,1,0:T(8,128)(2,1)}, bf16[2,512,512]{2,1,0:T(8,128)(2,1)}, u32[]{:S(2)}, u32[]{:S(2)}) %collective-permute-start.14) | collective-permute-done | bytes 1048608 | tf_op jit(solution)/shard_map/ppermute | solution.py:17
  623.6 63.3 %all-reduce.12.cloned.1.call-done = (bf16[64,4,128]{2,0,1:T(8,128)(2,1)}, bf16[64,4,128]{2,0,1:T(8,128)(2,1)}) async-done(((bf16[64,4,128]{2,0,1:T(8,128)(2,1)}, bf16[64,4,128]{2,0,1:T(8,128)(2,1)}), (bf16[64,4,128]{2,0,1:T(8,128)(2,1)}, bf16[64,4,128]{2,0,1:T(8,128)(2,1)})) %all-reduce.12.cloned.1.call-update) | async-done | bytes 131088
  703.6 171.3 %all-reduce.10.cloned.1.call-done = (f32[1024,512]{0,1:T(8,128)}, f32[1024,512]{0,1:T(8,128)}, f32[1024,512]{0,1:T(8,128)}, f32[512,1024]{1,0:T(8,128)}) async-done(((f32[1024,512]{0,1:T(8,128)}, f32[1024,512]{0,1:T(8,128)}, f32[1024,512]{0,1:T(8,128)}, f32[512,1024]{1,0:T(8,128)}), (f32[1024,512]{0,1:T(8,128)}, f32[1024,512]{0,1:T(8,128)}, f32[1024,512]{0,1:T(8,128)}, ...) | async-done | bytes 8388624 | tf_op jit(solution)/shard_map/psum | solution.py:286
  (309 shorter events, 283.2 us)
Async XLA Ops:
  7.2 679.7 %all-reduce.12.cloned.1.call-start = ((), (), s32[]{:S(2)}) async-start(), calls=%async_computation.1 | async-start | bytes 262144
  11.3 185.7 %collective-permute-start.7 = (bf16[1,512,512]{2,1,0:T(8,128)(2,1)}, bf16[1,512,512]{2,1,0:T(8,128)(2,1)}, u32[]{:S(2)}, u32[]{:S(2)}) collective-permute-start(bf16[1,512,512]{2,1,0:T(8,128)(2,1)} %bitcast.19), channel_id=1, source_target_pairs={{0,8},{1,9},{2,10},{3,11},{4,12},{5,13},{6,14},{7,15},{16,24},{17,... | collective-permute-start | bytes 1572872 | tf_op jit(solution)/shard_map/ppermute | solution.py:17
  18.1 43.3 %collective-permute-start.4 = (bf16[1,512,512]{2,1,0:T(8,128)(2,1)}, bf16[1,512,512]{2,1,0:T(8,128)(2,1)S(1)}, u32[]{:S(2)}, u32[]{:S(2)}) collective-permute-start(bf16[1,512,512]{2,1,0:T(8,128)(2,1)} %bitcast.19), channel_id=1, source_target_pairs={{0,1},{1,2},{2,3},{3,4},{4,5},{5,6},{6,7},{7,8},{8,9},{9,10},{10,1... | collective-permute-start | bytes 1572872 | tf_op jit(solution)/shard_map/ppermute | solution.py:17
  22.3 176.6 %collective-permute-start.3 = (bf16[1,512,512]{2,1,0:T(8,128)(2,1)S(1)}, bf16[1,512,512]{2,1,0:T(8,128)(2,1)}, u32[]{:S(2)}, u32[]{:S(2)}) collective-permute-start(bf16[1,512,512]{2,1,0:T(8,128)(2,1)S(1)} %bitcast.382), channel_id=1, source_target_pairs={{0,8},{1,9},{2,10},{3,11},{4,12},{5,13},{6,14},{7,15},{16,24},{17,... | collective-permute-start | bytes 1572872 | tf_op jit(solution)/shard_map/ppermute | solution.py:17
  24.4 45.4 %collective-permute-start = (bf16[1,512,512]{2,1,0:T(8,128)(2,1)S(1)}, bf16[1,512,512]{2,1,0:T(8,128)(2,1)}, u32[]{:S(2)}, u32[]{:S(2)}) collective-permute-start(bf16[1,512,512]{2,1,0:T(8,128)(2,1)S(1)} %bitcast.383), channel_id=1, source_target_pairs={{0,1},{1,2},{2,3},{3,4},{4,5},{5,6},{6,7},{7,8},{8,9},{9,10},{10,1... | collective-permute-start | bytes 1572872 | tf_op jit(solution)/shard_map/ppermute | solution.py:17
  62.7 35.5 %collective-permute-start.5 = (bf16[2,512,512]{2,1,0:T(8,128)(2,1)S(1)}, bf16[2,512,512]{2,1,0:T(8,128)(2,1)S(1)}, u32[]{:S(2)}, u32[]{:S(2)}) collective-permute-start(bf16[2,512,512]{2,1,0:T(8,128)(2,1)S(1)} %pad_maximum_fusion.3), channel_id=1, source_target_pairs={{0,2},{1,3},{2,4},{3,5},{4,6},{5,7},{6,8},{7,9},{8,10},{9,11},{10,... | collective-permute-start | bytes 3145736 | tf_op jit(solution)/shard_map/ppermute | solution.py:17
  71.9 119.7 %copy-start.50 = (u32[32]{0:T(128)S(1)}, u32[32]{0:T(128)}, u32[]{:S(2)}) copy-start(u32[32]{0:T(128)} %constant.355) | copy-start | bytes 388
  71.9 132.8 %collective-permute-start.1 = (bf16[2,512,512]{2,1,0:T(8,128)(2,1)}, bf16[2,512,512]{2,1,0:T(8,128)(2,1)}, u32[]{:S(2)}, u32[]{:S(2)}) collective-permute-start(bf16[2,512,512]{2,1,0:T(8,128)(2,1)} %pad_maximum_fusion.2), channel_id=1, source_target_pairs={{0,2},{1,3},{2,4},{3,5},{4,6},{5,7},{6,8},{7,9},{8,10},{9,11},{10,... | collective-permute-start | bytes 3145736 | tf_op jit(solution)/shard_map/ppermute | solution.py:17
  100.8 124.3 %collective-permute-start.6 = (bf16[4,512,512]{2,1,0:T(8,128)(2,1)}, bf16[4,512,512]{2,1,0:T(8,128)(2,1)}, u32[]{:S(2)}, u32[]{:S(2)}) collective-permute-start(bf16[4,512,512]{2,1,0:T(8,128)(2,1)} %pad_maximum_fusion.1), channel_id=1, source_target_pairs={{0,4},{1,5},{2,6},{3,7},{4,8},{5,9},{6,10},{7,11},{8,12},{9,13},{1... | collective-permute-start | bytes 6291464 | tf_op jit(solution)/shard_map/ppermute | solution.py:17
  127.2 64.9 %copy-start.22 = (bf16[4,128,4,128]{3,2,1,0:T(4,128)(2,1)}, bf16[4,128,4,128]{3,2,1,0:T(4,128)(2,1)S(1)}, u32[]{:S(2)}) copy-start(bf16[4,128,4,128]{3,2,1,0:T(4,128)(2,1)S(1)} %reshape.639) | copy-start | bytes 1572868
  207.6 58.5 %collective-permute-start.2 = (bf16[4,512,512]{2,1,0:T(8,128)(2,1)}, bf16[4,512,512]{2,1,0:T(8,128)(2,1)}, u32[]{:S(2)}, u32[]{:S(2)}) collective-permute-start(bf16[4,512,512]{2,1,0:T(8,128)(2,1)} %pad_maximum_fusion), channel_id=1, source_target_pairs={{0,4},{1,5},{2,6},{3,7},{4,8},{5,9},{6,10},{7,11},{8,12},{9,13},{1... | collective-permute-start | bytes 6291464 | tf_op jit(solution)/shard_map/ppermute | solution.py:17
  372.1 109.3 %collective-permute-start.8 = (bf16[1,512,512]{2,1,0:T(8,128)(2,1)}, bf16[1,512,512]{2,1,0:T(8,128)(2,1)}, u32[]{:S(2)}, u32[]{:S(2)}) collective-permute-start(bf16[1,512,512]{2,1,0:T(8,128)(2,1)} %convert_element_type.176), channel_id=1, source_target_pairs={{8,0},{9,1},{10,2},{11,3},{12,4},{13,5},{14,6},{15,7},{24,16},{25,... | collective-permute-start | bytes 1572872 | tf_op jit(solution)/shard_map/ppermute | solution.py:17
  392.4 96.8 %collective-permute-start.12 = (bf16[1,512,512]{2,1,0:T(8,128)(2,1)}, bf16[1,512,512]{2,1,0:T(8,128)(2,1)S(1)}, u32[]{:S(2)}, u32[]{:S(2)}) collective-permute-start(bf16[1,512,512]{2,1,0:T(8,128)(2,1)} %convert_element_type.185), channel_id=1, source_target_pairs={{8,0},{9,1},{10,2},{11,3},{12,4},{13,5},{14,6},{15,7},{24,16},{25,... | collective-permute-start | bytes 1572872 | tf_op jit(solution)/shard_map/ppermute | solution.py:17
  487.7 50.7 %collective-permute-start.9 = (bf16[4,512,512]{2,1,0:T(8,128)(2,1)}, bf16[4,512,512]{2,1,0:T(8,128)(2,1)}, u32[]{:S(2)}, u32[]{:S(2)}) collective-permute-start(bf16[4,512,512]{2,1,0:T(8,128)(2,1)} %slice.541), channel_id=1, source_target_pairs={{4,0},{5,1},{6,2},{7,3},{8,4},{9,5},{10,6},{11,7},{12,8},{13,9},{1... | collective-permute-start | bytes 6291464 | tf_op jit(solution)/shard_map/ppermute | solution.py:17
  494.1 89.2 %collective-permute-start.13 = (bf16[4,512,512]{2,1,0:T(8,128)(2,1)}, bf16[4,512,512]{2,1,0:T(8,128)(2,1)}, u32[]{:S(2)}, u32[]{:S(2)}) collective-permute-start(bf16[4,512,512]{2,1,0:T(8,128)(2,1)} %slice.540), channel_id=1, source_target_pairs={{4,0},{5,1},{6,2},{7,3},{8,4},{9,5},{10,6},{11,7},{12,8},{13,9},{1... | collective-permute-start | bytes 6291464 | tf_op jit(solution)/shard_map/ppermute | solution.py:17
  503.7 88.7 %copy-start.20 = (bf16[4,128,4,128]{3,2,1,0:T(4,128)(2,1)}, bf16[4,128,4,128]{3,2,1,0:T(4,128)(2,1)S(1)}, u32[]{:S(2)}) copy-start(bf16[4,128,4,128]{3,2,1,0:T(4,128)(2,1)S(1)} %copy.210) | copy-start | bytes 1572868
  543.3 49.1 %copy-start.36 = (bf16[1,512,1024]{2,1,0:T(8,128)(2,1)S(1)}, bf16[1,512,1024]{2,1,0:T(8,128)(2,1)}, u32[]{:S(2)}) copy-start(bf16[1,512,1024]{2,1,0:T(8,128)(2,1)} %param.29) | copy-start | bytes 3145732
  543.3 51.2 %collective-permute-start.10 = (bf16[2,512,512]{2,1,0:T(8,128)(2,1)}, bf16[2,512,512]{2,1,0:T(8,128)(2,1)}, u32[]{:S(2)}, u32[]{:S(2)}) collective-permute-start(bf16[2,512,512]{2,1,0:T(8,128)(2,1)} %slice.543), channel_id=1, source_target_pairs={{2,0},{3,1},{4,2},{5,3},{6,4},{7,5},{8,6},{9,7},{10,8},{11,9},{12,... | collective-permute-start | bytes 3145736 | tf_op jit(solution)/shard_map/ppermute | solution.py:17
  589.3 26.9 %collective-permute-start.14 = (bf16[2,512,512]{2,1,0:T(8,128)(2,1)}, bf16[2,512,512]{2,1,0:T(8,128)(2,1)}, u32[]{:S(2)}, u32[]{:S(2)}) collective-permute-start(bf16[2,512,512]{2,1,0:T(8,128)(2,1)} %slice.542), channel_id=1, source_target_pairs={{2,0},{3,1},{4,2},{5,3},{6,4},{7,5},{8,6},{9,7},{10,8},{11,9},{12,... | collective-permute-start | bytes 3145736 | tf_op jit(solution)/shard_map/ppermute | solution.py:17
  592.3 282.6 %all-reduce.10.cloned.1.call-start = ((), (), s32[]{:S(2)}) async-start(), calls=%async_computation | async-start | bytes 16777216 | tf_op jit(solution)/shard_map/psum | solution.py:286
  598.0 88.9 %copy-start.49 = (f32[4]{0:T(128)S(1)}, f32[4]{0:T(128)}, u32[]{:S(2)}) copy-start(f32[4]{0:T(128)} %get-tuple-element.184) | copy-start | bytes 52
  598.0 89.7 %collective-permute-start.11 = (bf16[1,512,512]{2,1,0:T(8,128)(2,1)}, bf16[1,512,512]{2,1,0:T(8,128)(2,1)}, u32[]{:S(2)}, u32[]{:S(2)}) collective-permute-start(bf16[1,512,512]{2,1,0:T(8,128)(2,1)} %slice.545), channel_id=1, source_target_pairs={{1,0},{2,1},{3,2},{4,3},{5,4},{6,5},{7,6},{8,7},{9,8},{10,9},{11,1... | collective-permute-start | bytes 1572872 | tf_op jit(solution)/shard_map/ppermute | solution.py:17
  619.1 68.8 %copy-start.46 = (pred[512]{0:T(512)(128)(4,1)S(1)}, pred[512]{0:T(512)(128)(4,1)}, u32[]{:S(2)}) copy-start(pred[512]{0:T(512)(128)(4,1)} %copy-done.45) | copy-start | bytes 1540
  620.0 67.7 %collective-permute-start.15 = (bf16[1,512,512]{2,1,0:T(8,128)(2,1)}, bf16[1,512,512]{2,1,0:T(8,128)(2,1)}, u32[]{:S(2)}, u32[]{:S(2)}) collective-permute-start(bf16[1,512,512]{2,1,0:T(8,128)(2,1)} %slice.544), channel_id=1, source_target_pairs={{1,0},{2,1},{3,2},{4,3},{5,4},{6,5},{7,6},{8,7},{9,8},{10,9},{11,1... | collective-permute-start | bytes 1572872 | tf_op jit(solution)/shard_map/ppermute | solution.py:17
  (47 other events, 565.7 us)
Sparse Core Ops, SparseCore 0:
  592.5 94.3 all-reduce.11
  694.2 180.7 all-reduce.9
where the time goes:
time: 903 us; the launch traced here: 892 us
  waiting for transfers between devices  318 us (35%)
  local copies, waits for them, and re-layouts  256 us (28%)
  blocking collectives  85.6 us (9%)
  starting transfers between devices  81 us (9%)
  matrix products  68.2 us (8%)
  other arithmetic  67.7 us (7%)
  between operations  16 us (2%)
    psum x1, waiting for transfers between devices, local(): lax.psum((weight_terms[0], weight_terms[1], weight_terms[2], weight_terms...  171 us
    ppermute x16, waiting for transfers between devices, shifted(): return lax.ppermute(block, axis, route)  83.1 us
    ppermute x16, starting transfers between devices, shifted(): return lax.ppermute(block, axis, route)  81 us
    unnamed x3, waiting for transfers between devices  63.4 us
    all_gather x1, blocking collectives, local(): lax.all_gather(own_summary[1], 'seq', axis=0, tiled=True)  63.2 us
    dot_general x19, matrix products, product(): return jnp.einsum(form, left, right, preferred_element_type=jnp.float32)  53.6 us
    unnamed x134, local copies, waits for them, and re-layouts  53.4 us
    dynamic_update_slice x6, local copies, waits for them, and re-layouts, spread(): lax.dynamic_update_slice_in_dim(running, current + grads[:, position], fi...  36.1 us
  transfers between devices with their start and end apart: 18, of which 5 were waited for; matrix products, arithmetic and copies ran while one was open for 29% of the time, Pallas kernels for 0%

commit v1 on v0

--- a/solution.py
+++ b/solution.py
@@ -9,6 +9,7 @@
 bar_offsets = (0, 1, 2, 4, 8, 12, 16, 24, 32)
 group_bars = 4
 far_score = -1e30
+reach_core = lambda unit: lax.psum(lax.psum(unit, "seq"), "dp")
 
 
 def shifted(block, axis, distance):
@@ -283,9 +284,7 @@
         product("td,te->de", inputs, grad_values),
         product("te,td->ed", attended_context, grad_out),
     )
-    summed = lax.psum(
-        (weight_terms[0], weight_terms[1], weight_terms[2], weight_terms[3]), ("dp", "seq")
-    )
+    summed = reach_core((weight_terms[0], weight_terms[1], weight_terms[2], weight_terms[3]))
     return (
         mixed[None],
         grad_in.astype(jnp.bfloat16)[None],

time: 903 us -> 1090 us (1.21)
  waiting for transfers between devices: 318 us -> 509 us
    psum x1 -> x2, waiting for transfers between devices: 171 us -> 363 us  [reach_core = lambda unit: lax.psum(lax.psum(unit, 'seq'), 'dp')]
    unnamed x3 -> x4, waiting for transfers between devices: 63.4 us -> 63.6 us
  transfers between devices with their start and end apart: 18 -> 19, of which waited for: 5 -> 6; matrix products, arithmetic and copies ran while one was open for 29% -> 24% of each run, Pallas kernels for 0% -> 0%
where the time goes in v1:
time: 1090 us; the launch traced here: 1080 us
  waiting for transfers between devices  509 us (47%)
  local copies, waits for them, and re-layouts  255 us (23%)
  blocking collectives  85.7 us (8%)
  starting transfers between devices  81.2 us (7%)
  matrix products  68.6 us (6%)
  other arithmetic  67.6 us (6%)
  between operations  15.7 us (1%)
    psum x2, waiting for transfers between devices, reach_core = lambda unit: lax.psum(lax.psum(unit, 'seq'), 'dp')  363 us
    ppermute x16, waiting for transfers between devices, shifted(): return lax.ppermute(block, axis, route)  82.9 us
    ppermute x16, starting transfers between devices, shifted(): return lax.ppermute(block, axis, route)  80.9 us
    unnamed x4, waiting for transfers between devices  63.6 us
    all_gather x1, blocking collectives, local(): lax.all_gather(own_summary[1], 'seq', axis=0, tiled=True)  63.2 us
    dot_general x19, matrix products, product(): return jnp.einsum(form, left, right, preferred_element_type=jnp.float32)  53.9 us
    unnamed x134, local copies, waits for them, and re-layouts  53.4 us
    dynamic_update_slice x6, local copies, waits for them, and re-layouts, spread(): lax.dynamic_update_slice_in_dim(running, current + grads[:, position], fi...  36 us
  transfers between devices with their start and end apart: 19, of which 6 were waited for; matrix products, arithmetic and copies ran while one was open for 24% of the time, Pallas kernels for 0%

profile of v1, /device:TPU:0, one launch (start us, length us, event | category | flops | bytes accessed | tf_op | source)
XLA Modules:
  0.0 1083.4 jit_solution(14594865241269398414)
XLA Ops:
  11.3 6.8 collective-permute-start.7
  36.8 22.5 %all-gather = bf16[16,4,512]{2,1,0:T(4,128)(2,1)S(1)} all-gather(bf16[1,4,512]{2,1,0:T(4,128)(2,1)S(1)} %get-tuple-element.213), channel_id=1, replica_groups=mesh['dp'=2,'seq'=16] {'seq'}, dimensions={0}, use_global_device_ids=true | all-gather | bytes 69632 | tf_op jit(solution)/shard_map/all_gather | solution.py:153
  71.9 26.4 %collective-permute-start.1 = (bf16[2,512,512]{2,1,0:T(8,128)(2,1)}, bf16[2,512,512]{2,1,0:T(8,128)(2,1)}, u32[]{:S(2)}, u32[]{:S(2)}) collective-permute-start(bf16[2,512,512]{2,1,0:T(8,128)(2,1)} %pad_maximum_fusion.2), channel_id=1, source_target_pairs={{0,2},{1,3},{2,4},{3,5},{4,6},{5,7},{6,8},{7,9},{8,10},{9,11},{10,... | collective-permute-start | bytes 3145736 | tf_op jit(solution)/shard_map/ppermute | solution.py:18
  100.8 20.4 %collective-permute-start.6 = (bf16[4,512,512]{2,1,0:T(8,128)(2,1)}, bf16[4,512,512]{2,1,0:T(8,128)(2,1)}, u32[]{:S(2)}, u32[]{:S(2)}) collective-permute-start(bf16[4,512,512]{2,1,0:T(8,128)(2,1)} %pad_maximum_fusion.1), channel_id=1, source_target_pairs={{0,4},{1,5},{2,6},{3,7},{4,8},{5,9},{6,10},{7,11},{8,12},{9,13},{1... | collective-permute-start | bytes 6291464 | tf_op jit(solution)/shard_map/ppermute | solution.py:18
  128.3 63.2 %all-gather.1 = bf16[16,4,512]{2,1,0:T(4,128)(2,1)S(1)} all-gather(bf16[1,4,512]{2,1,0:T(4,128)(2,1)S(1)} %get-tuple-element.212), channel_id=1, replica_groups=mesh['dp'=2,'seq'=16] {'seq'}, dimensions={0}, use_global_device_ids=true | all-gather | bytes 69632 | tf_op jit(solution)/shard_map/all_gather | solution.py:154
  234.9 8.0 reshape.634
  275.8 7.7 reshape.631
  306.9 6.9 multiply_reduce_fusion
  313.8 9.6 copy.235
  327.0 8.2 multiply_convert_fusion
  342.4 9.6 copy.221
  397.5 15.6 %copy.230 = f32[36,128,4,128]{3,2,1,0:T(4,128)} copy(f32[36,128,4,128]{3,1,2,0:T(8,128)} %constant_dynamic-update-slice_fusion.18) | data formatting | bytes 18874368 | tf_op jit(solution)/shard_map/while/body/eval_jaxpr/dynamic_update_slice | solution.py:125
  415.5 15.8 %copy.244 = f32[36,128,4,128]{3,2,1,0:T(4,128)} copy(f32[36,128,4,128]{3,1,2,0:T(8,128)} %constant_dynamic-update-slice_fusion.17) | data formatting | bytes 18874368 | tf_op jit(solution)/shard_map/while/body/eval_jaxpr/dynamic_update_slice | solution.py:125
  431.3 12.3 %reshape.642 = f32[9,512,512]{2,1,0:T(8,128)} reshape(f32[36,128,4,128]{3,2,1,0:T(4,128)} %copy.230) | data formatting | bytes 18874368 | tf_op jit(solution)/shard_map/reshape | solution.py:228
  443.6 8.4 rev.14
  457.5 12.3 %reshape.647 = f32[9,512,512]{2,1,0:T(8,128)} reshape(f32[36,128,4,128]{3,2,1,0:T(4,128)} %copy.244) | data formatting | bytes 18874368 | tf_op jit(solution)/shard_map/reshape | solution.py:229
  469.7 8.4 rev.15
  495.8 7.2 fusion.11
  510.8 27.6 %collective-permute-done.9 = bf16[4,512,512]{2,1,0:T(8,128)(2,1)} collective-permute-done((bf16[4,512,512]{2,1,0:T(8,128)(2,1)}, bf16[4,512,512]{2,1,0:T(8,128)(2,1)}, u32[]{:S(2)}, u32[]{:S(2)}) %collective-permute-start.9) | collective-permute-done | bytes 2097184 | tf_op jit(solution)/shard_map/ppermute | solution.py:18
  544.8 38.5 %collective-permute-done.13 = bf16[4,512,512]{2,1,0:T(8,128)(2,1)} collective-permute-done((bf16[4,512,512]{2,1,0:T(8,128)(2,1)}, bf16[4,512,512]{2,1,0:T(8,128)(2,1)}, u32[]{:S(2)}, u32[]{:S(2)}) %collective-permute-start.13) | collective-permute-done | bytes 2097184 | tf_op jit(solution)/shard_map/ppermute | solution.py:18
  599.4 16.8 %collective-permute-done.14 = bf16[2,512,512]{2,1,0:T(8,128)(2,1)} collective-permute-done((bf16[2,512,512]{2,1,0:T(8,128)(2,1)}, bf16[2,512,512]{2,1,0:T(8,128)(2,1)}, u32[]{:S(2)}, u32[]{:S(2)}) %collective-permute-start.14) | collective-permute-done | bytes 1048608 | tf_op jit(solution)/shard_map/ppermute | solution.py:18
  623.4 63.6 %all-reduce.16.cloned.1.call-done = (bf16[64,4,128]{2,0,1:T(8,128)(2,1)}, bf16[64,4,128]{2,0,1:T(8,128)(2,1)}) async-done(((bf16[64,4,128]{2,0,1:T(8,128)(2,1)}, bf16[64,4,128]{2,0,1:T(8,128)(2,1)}), (bf16[64,4,128]{2,0,1:T(8,128)(2,1)}, bf16[64,4,128]{2,0,1:T(8,128)(2,1)})) %all-reduce.16.cloned.1.call-update) | async-done | bytes 131088
  694.3 171.7 %all-reduce.12.cloned.1.call-done = (f32[1024,512]{0,1:T(8,128)}, f32[1024,512]{0,1:T(8,128)}, f32[1024,512]{0,1:T(8,128)}, f32[512,1024]{1,0:T(8,128)}) async-done(((f32[1024,512]{0,1:T(8,128)}, f32[1024,512]{0,1:T(8,128)}, f32[1024,512]{0,1:T(8,128)}, f32[512,1024]{1,0:T(8,128)}), (f32[1024,512]{0,1:T(8,128)}, f32[1024,512]{0,1:T(8,128)}, f32[1024,512]{0,1:T(8,128)}, ...) | async-done | bytes 8388624 | tf_op jit(solution)/shard_map/psum | solution.py:12
  875.6 191.0 %all-reduce.14.cloned.1.call-done = (f32[1024,512]{0,1:T(8,128)}, f32[1024,512]{0,1:T(8,128)}, f32[1024,512]{0,1:T(8,128)}, f32[512,1024]{1,0:T(8,128)}) async-done(((f32[1024,512]{0,1:T(8,128)}, f32[1024,512]{0,1:T(8,128)}, f32[1024,512]{0,1:T(8,128)}, f32[512,1024]{1,0:T(8,128)}), (f32[1024,512]{0,1:T(8,128)}, f32[1024,512]{0,1:T(8,128)}, f32[1024,512]{0,1:T(8,128)}, ...) | async-done | bytes 8388624 | tf_op jit(solution)/shard_map/psum | solution.py:12
  (312 shorter events, 289.4 us)
Async XLA Ops:
  7.2 679.7 %all-reduce.16.cloned.1.call-start = ((), (), s32[]{:S(2)}) async-start(), calls=%async_computation.2 | async-start | bytes 262144
  11.3 185.7 %collective-permute-start.7 = (bf16[1,512,512]{2,1,0:T(8,128)(2,1)}, bf16[1,512,512]{2,1,0:T(8,128)(2,1)}, u32[]{:S(2)}, u32[]{:S(2)}) collective-permute-start(bf16[1,512,512]{2,1,0:T(8,128)(2,1)} %bitcast.19), channel_id=1, source_target_pairs={{0,8},{1,9},{2,10},{3,11},{4,12},{5,13},{6,14},{7,15},{16,24},{17,... | collective-permute-start | bytes 1572872 | tf_op jit(solution)/shard_map/ppermute | solution.py:18
  18.1 43.3 %collective-permute-start.4 = (bf16[1,512,512]{2,1,0:T(8,128)(2,1)}, bf16[1,512,512]{2,1,0:T(8,128)(2,1)S(1)}, u32[]{:S(2)}, u32[]{:S(2)}) collective-permute-start(bf16[1,512,512]{2,1,0:T(8,128)(2,1)} %bitcast.19), channel_id=1, source_target_pairs={{0,1},{1,2},{2,3},{3,4},{4,5},{5,6},{6,7},{7,8},{8,9},{9,10},{10,1... | collective-permute-start | bytes 1572872 | tf_op jit(solution)/shard_map/ppermute | solution.py:18
  22.3 176.6 %collective-permute-start.3 = (bf16[1,512,512]{2,1,0:T(8,128)(2,1)S(1)}, bf16[1,512,512]{2,1,0:T(8,128)(2,1)}, u32[]{:S(2)}, u32[]{:S(2)}) collective-permute-start(bf16[1,512,512]{2,1,0:T(8,128)(2,1)S(1)} %bitcast.382), channel_id=1, source_target_pairs={{0,8},{1,9},{2,10},{3,11},{4,12},{5,13},{6,14},{7,15},{16,24},{17,... | collective-permute-start | bytes 1572872 | tf_op jit(solution)/shard_map/ppermute | solution.py:18
  24.4 45.4 %collective-permute-start = (bf16[1,512,512]{2,1,0:T(8,128)(2,1)S(1)}, bf16[1,512,512]{2,1,0:T(8,128)(2,1)}, u32[]{:S(2)}, u32[]{:S(2)}) collective-permute-start(bf16[1,512,512]{2,1,0:T(8,128)(2,1)S(1)} %bitcast.383), channel_id=1, source_target_pairs={{0,1},{1,2},{2,3},{3,4},{4,5},{5,6},{6,7},{7,8},{8,9},{9,10},{10,1... | collective-permute-start | bytes 1572872 | tf_op jit(solution)/shard_map/ppermute | solution.py:18
  62.7 35.5 %collective-permute-start.5 = (bf16[2,512,512]{2,1,0:T(8,128)(2,1)S(1)}, bf16[2,512,512]{2,1,0:T(8,128)(2,1)S(1)}, u32[]{:S(2)}, u32[]{:S(2)}) collective-permute-start(bf16[2,512,512]{2,1,0:T(8,128)(2,1)S(1)} %pad_maximum_fusion.3), channel_id=1, source_target_pairs={{0,2},{1,3},{2,4},{3,5},{4,6},{5,7},{6,8},{7,9},{8,10},{9,11},{10,... | collective-permute-start | bytes 3145736 | tf_op jit(solution)/shard_map/ppermute | solution.py:18
  71.9 119.7 %copy-start.50 = (u32[32]{0:T(128)S(1)}, u32[32]{0:T(128)}, u32[]{:S(2)}) copy-start(u32[32]{0:T(128)} %constant.355) | copy-start | bytes 388
  71.9 132.9 %collective-permute-start.1 = (bf16[2,512,512]{2,1,0:T(8,128)(2,1)}, bf16[2,512,512]{2,1,0:T(8,128)(2,1)}, u32[]{:S(2)}, u32[]{:S(2)}) collective-permute-start(bf16[2,512,512]{2,1,0:T(8,128)(2,1)} %pad_maximum_fusion.2), channel_id=1, source_target_pairs={{0,2},{1,3},{2,4},{3,5},{4,6},{5,7},{6,8},{7,9},{8,10},{9,11},{10,... | collective-permute-start | bytes 3145736 | tf_op jit(solution)/shard_map/ppermute | solution.py:18
  100.8 124.4 %collective-permute-start.6 = (bf16[4,512,512]{2,1,0:T(8,128)(2,1)}, bf16[4,512,512]{2,1,0:T(8,128)(2,1)}, u32[]{:S(2)}, u32[]{:S(2)}) collective-permute-start(bf16[4,512,512]{2,1,0:T(8,128)(2,1)} %pad_maximum_fusion.1), channel_id=1, source_target_pairs={{0,4},{1,5},{2,6},{3,7},{4,8},{5,9},{6,10},{7,11},{8,12},{9,13},{1... | collective-permute-start | bytes 6291464 | tf_op jit(solution)/shard_map/ppermute | solution.py:18
  127.2 64.9 %copy-start.22 = (bf16[4,128,4,128]{3,2,1,0:T(4,128)(2,1)}, bf16[4,128,4,128]{3,2,1,0:T(4,128)(2,1)S(1)}, u32[]{:S(2)}) copy-start(bf16[4,128,4,128]{3,2,1,0:T(4,128)(2,1)S(1)} %reshape.639) | copy-start | bytes 1572868
  207.6 58.4 %collective-permute-start.2 = (bf16[4,512,512]{2,1,0:T(8,128)(2,1)}, bf16[4,512,512]{2,1,0:T(8,128)(2,1)}, u32[]{:S(2)}, u32[]{:S(2)}) collective-permute-start(bf16[4,512,512]{2,1,0:T(8,128)(2,1)} %pad_maximum_fusion), channel_id=1, source_target_pairs={{0,4},{1,5},{2,6},{3,7},{4,8},{5,9},{6,10},{7,11},{8,12},{9,13},{1... | collective-permute-start | bytes 6291464 | tf_op jit(solution)/shard_map/ppermute | solution.py:18
  372.3 109.1 %collective-permute-start.8 = (bf16[1,512,512]{2,1,0:T(8,128)(2,1)}, bf16[1,512,512]{2,1,0:T(8,128)(2,1)}, u32[]{:S(2)}, u32[]{:S(2)}) collective-permute-start(bf16[1,512,512]{2,1,0:T(8,128)(2,1)} %convert_element_type.176), channel_id=1, source_target_pairs={{8,0},{9,1},{10,2},{11,3},{12,4},{13,5},{14,6},{15,7},{24,16},{25,... | collective-permute-start | bytes 1572872 | tf_op jit(solution)/shard_map/ppermute | solution.py:18
  392.6 96.8 %collective-permute-start.12 = (bf16[1,512,512]{2,1,0:T(8,128)(2,1)}, bf16[1,512,512]{2,1,0:T(8,128)(2,1)S(1)}, u32[]{:S(2)}, u32[]{:S(2)}) collective-permute-start(bf16[1,512,512]{2,1,0:T(8,128)(2,1)} %convert_element_type.185), channel_id=1, source_target_pairs={{8,0},{9,1},{10,2},{11,3},{12,4},{13,5},{14,6},{15,7},{24,16},{25,... | collective-permute-start | bytes 1572872 | tf_op jit(solution)/shard_map/ppermute | solution.py:18
  487.7 50.7 %collective-permute-start.9 = (bf16[4,512,512]{2,1,0:T(8,128)(2,1)}, bf16[4,512,512]{2,1,0:T(8,128)(2,1)}, u32[]{:S(2)}, u32[]{:S(2)}) collective-permute-start(bf16[4,512,512]{2,1,0:T(8,128)(2,1)} %slice.541), channel_id=1, source_target_pairs={{4,0},{5,1},{6,2},{7,3},{8,4},{9,5},{10,6},{11,7},{12,8},{13,9},{1... | collective-permute-start | bytes 6291464 | tf_op jit(solution)/shard_map/ppermute | solution.py:18
  494.3 89.0 %collective-permute-start.13 = (bf16[4,512,512]{2,1,0:T(8,128)(2,1)}, bf16[4,512,512]{2,1,0:T(8,128)(2,1)}, u32[]{:S(2)}, u32[]{:S(2)}) collective-permute-start(bf16[4,512,512]{2,1,0:T(8,128)(2,1)} %slice.540), channel_id=1, source_target_pairs={{4,0},{5,1},{6,2},{7,3},{8,4},{9,5},{10,6},{11,7},{12,8},{13,9},{1... | collective-permute-start | bytes 6291464 | tf_op jit(solution)/shard_map/ppermute | solution.py:18
  503.9 88.4 %copy-start.20 = (bf16[4,128,4,128]{3,2,1,0:T(4,128)(2,1)}, bf16[4,128,4,128]{3,2,1,0:T(4,128)(2,1)S(1)}, u32[]{:S(2)}) copy-start(bf16[4,128,4,128]{3,2,1,0:T(4,128)(2,1)S(1)} %copy.210) | copy-start | bytes 1572868
  543.3 51.2 %collective-permute-start.10 = (bf16[2,512,512]{2,1,0:T(8,128)(2,1)}, bf16[2,512,512]{2,1,0:T(8,128)(2,1)}, u32[]{:S(2)}, u32[]{:S(2)}) collective-permute-start(bf16[2,512,512]{2,1,0:T(8,128)(2,1)} %slice.543), channel_id=1, source_target_pairs={{2,0},{3,1},{4,2},{5,3},{6,4},{7,5},{8,6},{9,7},{10,8},{11,9},{12,... | collective-permute-start | bytes 3145736 | tf_op jit(solution)/shard_map/ppermute | solution.py:18
  589.3 26.9 %collective-permute-start.14 = (bf16[2,512,512]{2,1,0:T(8,128)(2,1)}, bf16[2,512,512]{2,1,0:T(8,128)(2,1)}, u32[]{:S(2)}, u32[]{:S(2)}) collective-permute-start(bf16[2,512,512]{2,1,0:T(8,128)(2,1)} %slice.542), channel_id=1, source_target_pairs={{2,0},{3,1},{4,2},{5,3},{6,4},{7,5},{8,6},{9,7},{10,8},{11,9},{12,... | collective-permute-start | bytes 3145736 | tf_op jit(solution)/shard_map/ppermute | solution.py:18
  592.3 273.7 %all-reduce.12.cloned.1.call-start = ((), (), s32[]{:S(2)}) async-start(), calls=%async_computation | async-start | bytes 16777216 | tf_op jit(solution)/shard_map/psum | solution.py:12
  598.0 88.9 %copy-start.49 = (f32[4]{0:T(128)S(1)}, f32[4]{0:T(128)}, u32[]{:S(2)}) copy-start(f32[4]{0:T(128)} %get-tuple-element.188) | copy-start | bytes 52
  598.0 89.7 %collective-permute-start.11 = (bf16[1,512,512]{2,1,0:T(8,128)(2,1)}, bf16[1,512,512]{2,1,0:T(8,128)(2,1)}, u32[]{:S(2)}, u32[]{:S(2)}) collective-permute-start(bf16[1,512,512]{2,1,0:T(8,128)(2,1)} %slice.545), channel_id=1, source_target_pairs={{1,0},{2,1},{3,2},{4,3},{5,4},{6,5},{7,6},{8,7},{9,8},{10,9},{11,1... | collective-permute-start | bytes 1572872 | tf_op jit(solution)/shard_map/ppermute | solution.py:18
  619.1 68.8 %copy-start.46 = (pred[512]{0:T(512)(128)(4,1)S(1)}, pred[512]{0:T(512)(128)(4,1)}, u32[]{:S(2)}) copy-start(pred[512]{0:T(512)(128)(4,1)} %copy-done.45) | copy-start | bytes 1540
  620.0 67.7 %collective-permute-start.15 = (bf16[1,512,512]{2,1,0:T(8,128)(2,1)}, bf16[1,512,512]{2,1,0:T(8,128)(2,1)}, u32[]{:S(2)}, u32[]{:S(2)}) collective-permute-start(bf16[1,512,512]{2,1,0:T(8,128)(2,1)} %slice.544), channel_id=1, source_target_pairs={{1,0},{2,1},{3,2},{4,3},{5,4},{6,5},{7,6},{8,7},{9,8},{10,9},{11,1... | collective-permute-start | bytes 1572872 | tf_op jit(solution)/shard_map/ppermute | solution.py:18
  694.1 372.5 %all-reduce.14.cloned.1.call-start = ((), (), s32[]{:S(2)}) async-start(), calls=%async_computation.1 | async-start | bytes 16777216 | tf_op jit(solution)/shard_map/psum | solution.py:12
  (48 other events, 614.9 us)
Sparse Core Ops, SparseCore 0:
  592.4 94.4 all-reduce.15
  694.2 171.7 all-reduce.11
  868.7 197.9 all-reduce.13
